TPU v7x, 32 devices: a whole 2x2x4 slice. The times are simulated.
32 devices in a mesh: patch: 8 (over y, x, core), rhs: 4 (over z).
Axes of the slice: x: 2, y: 2, z: 4, core: 2. Of those that a mesh axis runs over, the one named last changes fastest.
Arguments:
- rhs_vectors: float32 [64, 16, 384], P('patch', 'rhs'), may hold values from -8 to 8
- near_blocks: bfloat16 [64, 4, 384, 384], P('patch'), may hold values from -1 to 5, as said below
- neighbours: int32 [64, 4], P('patch'), may hold values from 0 to 63, as said below
- up_maps: float32 [64, 64, 384], P('patch'), may hold values from -0.3125 to 0.3125
- shift_up: float32 [64, 64, 64], P('patch'), may hold values from -0.25 to 0.25
- far_lists: int32 [8, 4], P('patch'), may hold values from 0 to 7, as said below
- translations: float32 [8, 4, 64, 64], P('patch'), may hold values from -0.375 to 0.375
- shift_down: float32 [64, 64, 64], P('patch'), may hold values from -0.75 to 0.75
- down_maps: float32 [64, 384, 64], P('patch'), may hold values from -0.375 to 0.375
Outputs:
- solution: float32 [64, 16, 384], P('patch', 'rhs')
- residual: float32 [64, 16, 384], P('patch', 'rhs')
Inputs may be any that keep to these rules, and one draw needn't show every extreme that they name: `neighbours`: entry 0 of each row is the patch itself; every other entry names a patch of the same cell or of the cell just before or just after it, cyclically. `far_lists`: entry 0 of each row names the cell just before or just after the row's own cell, cyclically, and for cell 0 the cell just before it; every other entry names a cell other than the row's own. `near_blocks`: the blocks keep the operator's symmetric part positive definite.
All inputs are finite; a program needn't handle non-finite values.
Results may differ from a plain program's by a relative error of at most 0.008.
The roundings to bfloat16 on the way count: a program that leaves them out, or rounds other values in their place, can miss the bound.
Values may be sent and summed in bfloat16 or wider, within the bound.
A program may use at most 64 MiB of HBM per device.

v0:
```python
import jax
import jax.numpy as jnp
from jax import lax
from jax.sharding import PartitionSpec as P

ITERS = 2
HIGH = lax.Precision.HIGHEST


def with_halo(block, sides, width):
    for axis, dim in sides:
        count = lax.axis_size(axis)
        forward = [(i, i + 1) for i in range(count - 1)]
        forward.append((count - 1, 0))
        backward = [(target, source) for source, target in forward]
        low = lax.ppermute(
            lax.slice_in_dim(block, block.shape[dim] - width, None, axis=dim), axis, forward
        )
        high = lax.ppermute(lax.slice_in_dim(block, 0, width, axis=dim), axis, backward)
        block = jnp.concatenate([low, block, high], axis=dim)
    return block


def spd_solve(matrix, right):
    factor = jnp.linalg.cholesky(matrix)
    return jax.scipy.linalg.cho_solve((factor, True), right)


def gram(left, right):
    return jnp.einsum("pkw,plw->kl", left, right, precision=HIGH)


def mix(field, coeffs):
    return jnp.einsum("pkw,kl->plw", field, coeffs, precision=HIGH)


def residual_sum(residual):
    return lax.psum(gram(residual, residual), "patch")


def apply_operator(
    field,
    near_blocks,
    neighbours,
    up_maps,
    shift_up,
    far_lists,
    translations,
    shift_down,
    down_maps,
):
    patches = field.shape[0]
    count = lax.axis_size("patch")
    first = lax.axis_index("patch") * patches - patches
    rounded = field.astype(jnp.bfloat16)
    widened = with_halo(rounded, (("patch", 0),), patches)
    local_ids = jnp.mod(neighbours - first, patches * count)
    picked = widened[local_ids]
    near = jnp.einsum("pjvw,pjkw->pkv", near_blocks, picked, preferred_element_type=jnp.float32)
    moments = jnp.einsum("pew,pkw->pke", up_maps, field, precision=HIGH)
    cell_moment = jnp.einsum("pfe,pke->kf", shift_up, moments, precision=HIGH)
    sources = far_lists[0]
    table = translations[0]
    piece = lax.all_gather(cell_moment[None], "patch", axis=0, tiled=True)
    labels = jnp.arange(piece.shape[0], dtype=jnp.int32)
    select = (sources[:, None] == labels[None, :]).astype(jnp.float32)
    chosen = jnp.einsum("ji,ike->jke", select, piece, precision=HIGH)
    local_exp = jnp.zeros_like(cell_moment) + jnp.einsum(
        "jfe,jke->kf", table, chosen, precision=HIGH
    )
    patch_exp = jnp.einsum("pfe,ke->pkf", shift_down, local_exp, precision=HIGH)
    far = jnp.einsum("pvf,pkf->pkv", down_maps, patch_exp, precision=HIGH)
    return near + far


def on_device(
    rhs_vectors,
    near_blocks,
    neighbours,
    up_maps,
    shift_up,
    far_lists,
    translations,
    shift_down,
    down_maps,
):
    my_cols = rhs_vectors.shape[1]
    offset = lax.axis_index("rhs") * my_cols
    residual = lax.all_gather(rhs_vectors, "rhs", axis=1, tiled=True)
    solution = jnp.zeros_like(residual)
    direction = residual
    current = jnp.zeros((residual.shape[1], residual.shape[1]), jnp.float32)
    for step in range(ITERS):
        image = apply_operator(
            direction,
            near_blocks,
            neighbours,
            up_maps,
            shift_up,
            far_lists,
            translations,
            shift_down,
            down_maps,
        )
        if step == 0:
            current = residual_sum(residual)
        curve = lax.psum(gram(direction, image), "patch")
        curve = 0.5 * (curve + curve.T)
        alpha = spd_solve(curve, current)
        solution = solution + mix(direction, alpha)
        residual = residual - mix(image, alpha)
        if step + 1 < ITERS:
            following = residual_sum(residual)
            beta = spd_solve(current, following)
            direction = residual + mix(direction, beta)
            current = following
    solution_mine = lax.dynamic_slice_in_dim(solution, offset, my_cols, 1)
    residual_mine = lax.dynamic_slice_in_dim(residual, offset, my_cols, 1)
    return (solution_mine, residual_mine)


def solution(mesh):
    return jax.shard_map(
        on_device,
        mesh=mesh,
        in_specs=(
            P("patch", "rhs", None),
            P("patch", None, None, None),
            P("patch", None),
            P("patch", None, None),
            P("patch", None, None),
            P("patch", None),
            P("patch", None, None, None),
            P("patch", None, None),
            P("patch", None, None),
        ),
        out_specs=(P("patch", "rhs", None), P("patch", "rhs", None)),
        check_vma=False,
    )
```

profile of v0, /device:TPU:0, one launch (start us, length us, event | category | flops | bytes accessed | tf_op | source)
XLA Modules:
  0.0 129.5 jit_solution(5300560113778208520)
XLA Ops:
  0.6 0.9 copy.61
  1.5 15.5 %all_gather.9 = f32[8,16,384]{2,0,1:T(8,128)S(1)} all-gather(f32[8,4,384]{2,0,1:T(8,128)S(1)} %copy.61), channel_id=1, replica_groups=mesh['patch'=8,'rhs'=4] {'rhs'}, dimensions={1}, use_global_device_ids=true | all-gather | bytes 245760 | tf_op jit(solution)/shard_map/all_gather | solution.py:89
  17.1 0.5 collective-permute-start
  17.6 0.4 convolution_bitcast_fusion.14
  17.9 0.7 compare_select_fusion
  18.8 2.1 %fusion.11 = f32[8,16,64]{2,1,0:T(8,128)S(1)} fusion(f32[8,64,384]{2,1,0:T(8,128)} %param.15, f32[8,16,384]{2,0,1:T(8,128)S(1)} %all_gather.9), kind=kOutput, calls=%fused_computation.33 | convolution fusion | flops 37748736 | bytes 1015808 | tf_op jit(solution)/shard_map/pew,pkw->pke/dot_general | solution.py:60
  20.9 1.2 convolution_bitcast_fusion.11
  22.1 9.3 %all-gather = f32[128,64]{1,0:T(8,128)S(1)} all-gather(f32[16,64]{1,0:T(8,128)S(1)} %convolution_bitcast_fusion.11), channel_id=2, replica_groups=mesh['patch'=8,'rhs'=4] {'patch'}, dimensions={0}, use_global_device_ids=true | all-gather | bytes 36864 | tf_op jit(solution)/shard_map/all_gather | solution.py:64
  31.4 0.9 fusion.15
  32.3 1.1 fusion.4
  33.4 1.7 %convolution_bitcast_fusion.6 = f32[8,16,64]{2,1,0:T(8,128)S(1)} fusion(f32[16,64,1]{1,0,2:T(8,128)S(1)} %fusion.4, f32[8,64,64]{2,1,0:T(8,128)} %param.19), kind=kOutput, calls=%fused_computation.12 | convolution fusion | flops 6291456 | bytes 167936 | tf_op jit(solution)/shard_map/pfe,ke->pkf/dot_general | solution.py:71
  35.2 0.6 gather_fusion
  35.9 6.3 %convolution_bitcast_fusion.4 = f32[8,16,384]{2,1,0:T(8,128)S(1)} fusion(bf16[8,4,16,384]{3,2,1,0:T(8,128)(2,1)S(1)} %bitcast.140, bf16[8,4,384,384]{3,2,1,0:T(8,128)(2,1)} %param.13), kind=kOutput, calls=%fused_computation.10 | convolution fusion | flops 150994944 | bytes 10027008 | tf_op jit(solution)/shard_map/pjvw,pjkw->pkv/dot_general | solution.py:59
  42.2 0.6 convolution_add_fusion.1
  42.8 0.4 convolution_bitcast_fusion.15
  43.2 23.6 %all-reduce = (f32[16,16]{0,1:T(8,128)S(1)}, f32[16,16]{1,0:T(8,128)S(1)}) all-reduce(f32[16,16]{0,1:T(8,128)S(1)} %convolution_bitcast_fusion.14, f32[16,16]{1,0:T(8,128)S(1)} %convolution_bitcast_fusion.15), channel_id=1, replica_groups=mesh['patch'=8,'rhs'=4] {'patch'}, use_global_device_ids=true, to_apply=%region_3.5 | all-reduce | flops 512 | bytes 4096 | tf_op jit(solution)/shard_map/psum | solution.py:38
  67.0 1.5 %cholesky.59 = f32[16,16]{1,0:T(8,128)S(1)} custom-call(f32[16,16]{1,0:T(8,128)S(1)} %fusion.35), custom_call_target="Cholesky" | custom-call | tf_op jit(solution)/shard_map/jit(cholesky)/cholesky | solution.py:25
  68.4 0.6 compare_reduce_fusion.2
  69.1 0.6 fusion.20
  69.8 1.2 custom-call.9
  71.5 0.3 fusion.1
  71.8 0.3 convolution_bitcast_fusion.13
  72.1 12.1 %psum.30 = f32[16,16]{1,0:T(8,128)S(1)} all-reduce(f32[16,16]{1,0:T(8,128)S(1)} %convolution_bitcast_fusion.13), channel_id=1, replica_groups=mesh['patch'=8,'rhs'=4] {'patch'}, use_global_device_ids=true, to_apply=%region_4.7 | all-reduce | flops 256 | bytes 2048 | tf_op jit(solution)/shard_map/psum | solution.py:38
  84.2 1.4 %cholesky.70 = f32[16,16]{1,0:T(8,128)S(1)} custom-call(f32[16,16]{1,0:T(8,128)S(1)} %fusion.31), custom_call_target="Cholesky" | custom-call | tf_op jit(solution)/shard_map/jit(cholesky)/cholesky | solution.py:25
  85.7 0.6 compare_reduce_fusion.1
  86.3 0.6 fusion.21
  87.0 1.2 custom-call.10
  88.6 0.3 fusion.43
  89.0 0.5 collective-permute-start.2
  89.5 0.3 fusion.7
  89.8 0.9 fusion.44
  90.8 0.3 convolution_bitcast_fusion.8
  91.1 9.4 %all-gather.1 = f32[128,64]{1,0:T(8,128)S(1)} all-gather(f32[16,64]{1,0:T(8,128)S(1)} %convolution_bitcast_fusion.8), channel_id=3, replica_groups=mesh['patch'=8,'rhs'=4] {'patch'}, dimensions={0}, use_global_device_ids=true | all-gather | bytes 36864 | tf_op jit(solution)/shard_map/all_gather | solution.py:64
  100.4 0.2 fusion.13
  100.9 0.7 convolution_bitcast_fusion.5
  101.7 0.6 gather_fusion.1
  102.3 6.2 %convolution_bitcast_fusion.3 = f32[8,16,384]{2,1,0:T(8,128)S(1)} fusion(bf16[8,4,16,384]{3,2,1,0:T(8,128)(2,1)S(1)} %bitcast.139, bf16[8,4,384,384]{3,2,1,0:T(8,128)(2,1)} %param.13), kind=kOutput, calls=%fused_computation.9 | convolution fusion | flops 150994944 | bytes 10027008 | tf_op jit(solution)/shard_map/pjvw,pjkw->pkv/dot_general | solution.py:59
  108.5 0.6 convolution_add_fusion
  109.2 0.3 convolution_bitcast_fusion.12
  109.5 13.5 %psum.31 = f32[16,16]{1,0:T(8,128)S(1)} all-reduce(f32[16,16]{1,0:T(8,128)S(1)} %convolution_bitcast_fusion.12), channel_id=1, replica_groups=mesh['patch'=8,'rhs'=4] {'patch'}, use_global_device_ids=true, to_apply=%region_5.8 | all-reduce | flops 256 | bytes 2048 | tf_op jit(solution)/shard_map/psum | solution.py:107
  123.1 1.5 %cholesky.81 = f32[16,16]{1,0:T(8,128)S(1)} custom-call(f32[16,16]{1,0:T(8,128)S(1)} %fusion.26), custom_call_target="Cholesky" | custom-call | tf_op jit(solution)/shard_map/jit(cholesky)/cholesky | solution.py:25
  124.6 0.6 compare_reduce_fusion
  125.3 0.6 fusion.22
  125.9 1.2 custom-call.11
  127.6 0.3 fusion.45
  127.9 0.3 convolution_bitcast_fusion
  128.2 0.6 dynamic-slice_subtract_fusion
  128.8 0.6 fusion.17
  (44 shorter events, 2.4 us)
Async XLA Ops:
  0.6 41.6 %copy-start = (f32[8,384,64]{1,2,0:T(8,128)S(1)}, f32[8,384,64]{1,2,0:T(8,128)}, u32[]{:S(2)}) copy-start(f32[8,384,64]{1,2,0:T(8,128)} %param.20) | copy-start | bytes 2359300
  17.0 18.1 %collective-permute-start.1 = (bf16[8,16,384]{2,1,0:T(8,128)(2,1)S(1)}, bf16[8,16,384]{2,1,0:T(8,128)(2,1)S(1)}, u32[]{:S(2)}, u32[]{:S(2)}) collective-permute-start(bf16[8,16,384]{2,1,0:T(8,128)(2,1)S(1)} %copy.116), channel_id=1, source_target_pairs={{4,0},{8,4},{12,8},{16,12},{20,16},{24,20},{28,24},{0,28},{5,1},{9... | collective-permute-start | bytes 294920 | tf_op jit(solution)/shard_map/ppermute | solution.py:19
  17.1 18.1 %collective-permute-start = (bf16[8,16,384]{2,1,0:T(8,128)(2,1)S(1)}, bf16[8,16,384]{2,1,0:T(8,128)(2,1)S(1)}, u32[]{:S(2)}, u32[]{:S(2)}) collective-permute-start(bf16[8,16,384]{2,1,0:T(8,128)(2,1)S(1)} %copy.116), channel_id=1, source_target_pairs={{0,4},{4,8},{8,12},{12,16},{16,20},{20,24},{24,28},{28,0},{1,5},{5... | collective-permute-start | bytes 294920 | tf_op jit(solution)/shard_map/ppermute | solution.py:16
  35.8 54.0 %copy-start.1 = (f32[8,64,384]{2,1,0:T(8,128)S(1)}, f32[8,64,384]{2,1,0:T(8,128)}, u32[]{:S(2)}) copy-start(f32[8,64,384]{2,1,0:T(8,128)} %param.15) | copy-start | bytes 2359300
  35.9 54.9 %copy-start.2 = (f32[8,64,64]{2,1,0:T(8,128)S(1)}, f32[8,64,64]{2,1,0:T(8,128)}, u32[]{:S(2)}) copy-start(f32[8,64,64]{2,1,0:T(8,128)} %param.16) | copy-start | bytes 393220
  35.9 64.6 %copy-start.5 = (s32[1,4]{1,0:T(1,128)S(1)}, s32[1,4]{1,0:T(1,128)}, u32[]{:S(2)}) copy-start(s32[1,4]{1,0:T(1,128)} %param.17) | copy-start | bytes 52
  35.9 64.8 %copy-start.4 = (f32[1,4,64,64]{3,2,1,0:T(8,128)S(1)}, f32[1,4,64,64]{3,2,1,0:T(8,128)}, u32[]{:S(2)}) copy-start(f32[1,4,64,64]{3,2,1,0:T(8,128)} %param.18) | copy-start | bytes 196612
  35.9 65.0 %copy-start.3 = (f32[8,64,64]{2,1,0:T(8,128)S(1)}, f32[8,64,64]{2,1,0:T(8,128)}, u32[]{:S(2)}) copy-start(f32[8,64,64]{2,1,0:T(8,128)} %param.19) | copy-start | bytes 393220
  89.0 12.6 %collective-permute-start.3 = (bf16[8,16,384]{2,1,0:T(8,128)(2,1)S(1)}, bf16[8,16,384]{2,1,0:T(8,128)(2,1)S(1)}, u32[]{:S(2)}, u32[]{:S(2)}) collective-permute-start(bf16[8,16,384]{2,1,0:T(8,128)(2,1)S(1)} %get-tuple-element.6), channel_id=1, source_target_pairs={{4,0},{8,4},{12,8},{16,12},{20,16},{24,20},{28,24},{0,28},{5,1},{9... | collective-permute-start | bytes 294920 | tf_op jit(solution)/shard_map/ppermute | solution.py:19
  89.0 12.6 %collective-permute-start.2 = (bf16[8,16,384]{2,1,0:T(8,128)(2,1)S(1)}, bf16[8,16,384]{2,1,0:T(8,128)(2,1)S(1)}, u32[]{:S(2)}, u32[]{:S(2)}) collective-permute-start(bf16[8,16,384]{2,1,0:T(8,128)(2,1)S(1)} %get-tuple-element.6), channel_id=1, source_target_pairs={{0,4},{4,8},{8,12},{12,16},{16,20},{20,24},{24,28},{28,0},{1,5},{5... | collective-permute-start | bytes 294920 | tf_op jit(solution)/shard_map/ppermute | solution.py:16
where the time goes:
time: 130 us; the launch traced here: 129 us
  blocking collectives  83.3 us (64%)
  matrix products  27.2 us (21%)
  other arithmetic  14.2 us (11%)
  local copies, waits for them, and re-layouts  2.76 us (2%)
    psum x2, blocking collectives, residual_sum(): return lax.psum(gram(residual, residual), 'patch')  35.7 us
    all_gather x2, blocking collectives, apply_operator(): piece = lax.all_gather(cell_moment[None], 'patch', axis=0, tiled=True)  18.7 us
    all_gather x1, blocking collectives, on_device(): residual = lax.all_gather(rhs_vectors, 'rhs', axis=1, tiled=True)  15.5 us
    psum x1, blocking collectives, on_device(): curve = lax.psum(gram(direction, image), 'patch')  13.5 us
    dot_general x2, matrix products, apply_operator(): jnp.einsum('pjvw,pjkw->pkv', near_blocks, picked, preferred_element_type=...  12.5 us
    another operation x9, other arithmetic, spd_solve(): factor = jnp.linalg.cholesky(matrix)  6.39 us
    another operation x6, other arithmetic, spd_solve(): return jax.scipy.linalg.cho_solve((factor, True), right)  5.63 us
    dot_general x2, matrix products, apply_operator(): moments = jnp.einsum('pew,pkw->pke', up_maps, field, precision=HIGH)  2.99 us
  transfers between devices with their start and end apart: 4, of which 0 were waited for; matrix products, arithmetic and copies ran while one was open for 8% of the time, Pallas kernels for 0%

commit v1 on v0

--- a/solution.py
+++ b/solution.py
@@ -104,7 +104,7 @@
         )
         if step == 0:
             current = residual_sum(residual)
-        curve = lax.psum(gram(direction, image), "patch")
+        curve = jnp.sum(lax.all_gather(gram(direction, image), "patch"), axis=0)
         curve = 0.5 * (curve + curve.T)
         alpha = spd_solve(curve, current)
         solution = solution + mix(direction, alpha)

time: 130 us -> 126 us (0.969)
  blocking collectives: 83.3 us -> 78.9 us
    all_gather x0 -> x2, blocking collectives: none -> 17.1 us  [on_device(): curve = jnp.sum(lax.all_gather(gram(direction, image), 'patch'), axis=0)]
    psum x1 -> x0, blocking collectives: 13.5 us -> none  [on_device(): curve = lax.psum(gram(direction, image), 'patch')]
    psum x2, blocking collectives: 35.7 us -> 27.7 us  [residual_sum(): return lax.psum(gram(residual, residual), 'patch')]
  transfers between devices with their start and end apart: 4 -> 4, of which waited for: 0 -> 0; matrix products, arithmetic and copies ran while one was open for 8% -> 12% of each run, Pallas kernels for 0% -> 0%
where the time goes in v1:
time: 126 us; the launch traced here: 125 us
  blocking collectives  78.9 us (63%)
  matrix products  27.2 us (22%)
  other arithmetic  14.2 us (11%)
  local copies, waits for them, and re-layouts  2.84 us (2%)
    psum x2, blocking collectives, residual_sum(): return lax.psum(gram(residual, residual), 'patch')  27.7 us
    all_gather x2, blocking collectives, apply_operator(): piece = lax.all_gather(cell_moment[None], 'patch', axis=0, tiled=True)  18.6 us
    all_gather x2, blocking collectives, on_device(): curve = jnp.sum(lax.all_gather(gram(direction, image), 'patch'), axis=0)  17.1 us
    all_gather x1, blocking collectives, on_device(): residual = lax.all_gather(rhs_vectors, 'rhs', axis=1, tiled=True)  15.5 us
    dot_general x2, matrix products, apply_operator(): jnp.einsum('pjvw,pjkw->pkv', near_blocks, picked, preferred_element_type=...  12.5 us
    another operation x9, other arithmetic, spd_solve(): factor = jnp.linalg.cholesky(matrix)  6.39 us
    another operation x6, other arithmetic, spd_solve(): return jax.scipy.linalg.cho_solve((factor, True), right)  5.63 us
    dot_general x2, matrix products, apply_operator(): moments = jnp.einsum('pew,pkw->pke', up_maps, field, precision=HIGH)  2.99 us
  transfers between devices with their start and end apart: 4, of which 0 were waited for; matrix products, arithmetic and copies ran while one was open for 12% of the time, Pallas kernels for 0%

profile of v1, /device:TPU:0, one launch (start us, length us, event | category | flops | bytes accessed | tf_op | source)
XLA Modules:
  0.0 125.2 jit_solution(2006733811853276596)
XLA Ops:
  0.6 0.9 copy.60
  1.5 15.5 %all_gather.21 = f32[8,16,384]{2,0,1:T(8,128)S(1)} all-gather(f32[8,4,384]{2,0,1:T(8,128)S(1)} %copy.60), channel_id=1, replica_groups=mesh['patch'=8,'rhs'=4] {'rhs'}, dimensions={1}, use_global_device_ids=true | all-gather | bytes 245760 | tf_op jit(solution)/shard_map/all_gather | solution.py:89
  17.1 0.5 collective-permute-start
  17.6 0.4 convolution_bitcast_fusion.14
  17.9 14.3 %psum.14 = f32[16,16]{0,1:T(8,128)S(1)} all-reduce(f32[16,16]{0,1:T(8,128)S(1)} %convolution_bitcast_fusion.14), channel_id=1, replica_groups=mesh['patch'=8,'rhs'=4] {'patch'}, use_global_device_ids=true, to_apply=%region_3.5 | all-reduce | flops 256 | bytes 2048 | tf_op jit(solution)/shard_map/psum | solution.py:38
  32.2 0.7 compare_select_fusion
  33.1 2.1 %fusion.11 = f32[8,16,64]{2,1,0:T(8,128)S(1)} fusion(f32[8,64,384]{2,1,0:T(8,128)} %param.15, f32[8,16,384]{2,0,1:T(8,128)S(1)} %all_gather.21), kind=kOutput, calls=%fused_computation.33 | convolution fusion | flops 37748736 | bytes 1015808 | tf_op jit(solution)/shard_map/pew,pkw->pke/dot_general | solution.py:60
  35.1 1.2 convolution_bitcast_fusion.11
  36.4 9.3 %all-gather = f32[128,64]{1,0:T(8,128)S(1)} all-gather(f32[16,64]{1,0:T(8,128)S(1)} %convolution_bitcast_fusion.11), channel_id=2, replica_groups=mesh['patch'=8,'rhs'=4] {'patch'}, dimensions={0}, use_global_device_ids=true | all-gather | bytes 36864 | tf_op jit(solution)/shard_map/all_gather | solution.py:64
  45.7 1.5 %cholesky.70 = f32[16,16]{1,0:T(8,128)S(1)} custom-call(f32[16,16]{1,0:T(8,128)S(1)} %fusion.31), custom_call_target="Cholesky" | custom-call | tf_op jit(solution)/shard_map/jit(cholesky)/cholesky | solution.py:25
  47.2 0.6 compare_reduce_fusion.1
  47.9 0.6 fusion.21
  48.5 1.2 custom-call.10
  49.8 0.9 fusion.15
  50.6 1.1 fusion.4
  51.7 1.7 %convolution_bitcast_fusion.6 = f32[8,16,64]{2,1,0:T(8,128)S(1)} fusion(f32[16,64,1]{1,0,2:T(8,128)S(1)} %fusion.4, f32[8,64,64]{2,1,0:T(8,128)} %param.19), kind=kOutput, calls=%fused_computation.12 | convolution fusion | flops 6291456 | bytes 167936 | tf_op jit(solution)/shard_map/pfe,ke->pkf/dot_general | solution.py:71
  53.5 0.6 gather_fusion
  54.2 6.3 %convolution_bitcast_fusion.4 = f32[8,16,384]{2,1,0:T(8,128)S(1)} fusion(bf16[8,4,16,384]{3,2,1,0:T(8,128)(2,1)S(1)} %bitcast.142, bf16[8,4,384,384]{3,2,1,0:T(8,128)(2,1)} %param.13), kind=kOutput, calls=%fused_computation.10 | convolution fusion | flops 150994944 | bytes 10027008 | tf_op jit(solution)/shard_map/pjvw,pjkw->pkv/dot_general | solution.py:59
  60.6 0.6 convolution_add_fusion.1
  61.2 0.4 convolution_bitcast_fusion.15
  61.6 8.3 %all-gather.1 = f32[128,16]{1,0:T(8,128)S(1)} all-gather(f32[16,16]{1,0:T(8,128)S(1)} %copy.67), channel_id=3, replica_groups=mesh['patch'=8,'rhs'=4] {'patch'}, dimensions={0}, use_global_device_ids=true | all-gather | bytes 9216 | tf_op jit(solution)/shard_map/all_gather | solution.py:107
  70.1 1.5 %cholesky.59 = f32[16,16]{1,0:T(8,128)S(1)} custom-call(f32[16,16]{1,0:T(8,128)S(1)} %fusion.35), custom_call_target="Cholesky" | custom-call | tf_op jit(solution)/shard_map/jit(cholesky)/cholesky | solution.py:25
  71.6 0.6 compare_reduce_fusion.2
  72.2 0.6 fusion.20
  72.9 1.2 custom-call.9
  74.5 0.3 fusion.1
  74.8 0.3 convolution_bitcast_fusion.13
  75.2 13.5 %psum.15 = f32[16,16]{1,0:T(8,128)S(1)} all-reduce(f32[16,16]{1,0:T(8,128)S(1)} %convolution_bitcast_fusion.13), channel_id=1, replica_groups=mesh['patch'=8,'rhs'=4] {'patch'}, use_global_device_ids=true, to_apply=%region_4.7 | all-reduce | flops 256 | bytes 2048 | tf_op jit(solution)/shard_map/psum | solution.py:38
  89.0 0.3 fusion.43
  89.4 0.5 collective-permute-start.2
  89.9 0.3 fusion.7
  90.2 0.9 fusion.44
  91.2 0.3 convolution_bitcast_fusion.8
  91.5 9.3 %all-gather.2 = f32[128,64]{1,0:T(8,128)S(1)} all-gather(f32[16,64]{1,0:T(8,128)S(1)} %convolution_bitcast_fusion.8), channel_id=4, replica_groups=mesh['patch'=8,'rhs'=4] {'patch'}, dimensions={0}, use_global_device_ids=true | all-gather | bytes 36864 | tf_op jit(solution)/shard_map/all_gather | solution.py:64
  101.2 0.7 convolution_bitcast_fusion.5
  102.0 0.6 gather_fusion.1
  102.7 6.2 %convolution_bitcast_fusion.3 = f32[8,16,384]{2,1,0:T(8,128)S(1)} fusion(bf16[8,4,16,384]{3,2,1,0:T(8,128)(2,1)S(1)} %bitcast.141, bf16[8,4,384,384]{3,2,1,0:T(8,128)(2,1)} %param.13), kind=kOutput, calls=%fused_computation.9 | convolution fusion | flops 150994944 | bytes 10027008 | tf_op jit(solution)/shard_map/pjvw,pjkw->pkv/dot_general | solution.py:59
  108.9 0.6 convolution_add_fusion
  109.5 0.3 convolution_bitcast_fusion.12
  109.8 8.9 %all-gather.3 = f32[128,16]{1,0:T(8,128)S(1)} all-gather(f32[16,16]{1,0:T(8,128)S(1)} %convolution_bitcast_fusion.12), channel_id=5, replica_groups=mesh['patch'=8,'rhs'=4] {'patch'}, dimensions={0}, use_global_device_ids=true | all-gather | bytes 9216 | tf_op jit(solution)/shard_map/all_gather | solution.py:107
  118.9 1.5 %cholesky.81 = f32[16,16]{1,0:T(8,128)S(1)} custom-call(f32[16,16]{1,0:T(8,128)S(1)} %fusion.26), custom_call_target="Cholesky" | custom-call | tf_op jit(solution)/shard_map/jit(cholesky)/cholesky | solution.py:25
  120.4 0.6 compare_reduce_fusion
  121.0 0.6 fusion.22
  121.7 1.2 custom-call.11
  123.3 0.3 fusion.45
  123.6 0.3 convolution_bitcast_fusion
  123.9 0.6 dynamic-slice_subtract_fusion
  124.6 0.6 fusion.17
  (48 shorter events, 2.7 us)
Async XLA Ops:
  0.6 59.9 %copy-start = (f32[8,384,64]{1,2,0:T(8,128)S(1)}, f32[8,384,64]{1,2,0:T(8,128)}, u32[]{:S(2)}) copy-start(f32[8,384,64]{1,2,0:T(8,128)} %param.20) | copy-start | bytes 2359300
  17.0 36.5 %collective-permute-start.1 = (bf16[8,16,384]{2,1,0:T(8,128)(2,1)S(1)}, bf16[8,16,384]{2,1,0:T(8,128)(2,1)S(1)}, u32[]{:S(2)}, u32[]{:S(2)}) collective-permute-start(bf16[8,16,384]{2,1,0:T(8,128)(2,1)S(1)} %copy.115), channel_id=1, source_target_pairs={{4,0},{8,4},{12,8},{16,12},{20,16},{24,20},{28,24},{0,28},{5,1},{9... | collective-permute-start | bytes 294920 | tf_op jit(solution)/shard_map/ppermute | solution.py:19
  17.1 36.4 %collective-permute-start = (bf16[8,16,384]{2,1,0:T(8,128)(2,1)S(1)}, bf16[8,16,384]{2,1,0:T(8,128)(2,1)S(1)}, u32[]{:S(2)}, u32[]{:S(2)}) collective-permute-start(bf16[8,16,384]{2,1,0:T(8,128)(2,1)S(1)} %copy.115), channel_id=1, source_target_pairs={{0,4},{4,8},{8,12},{12,16},{16,20},{20,24},{24,28},{28,0},{1,5},{5... | collective-permute-start | bytes 294920 | tf_op jit(solution)/shard_map/ppermute | solution.py:16
  54.2 36.1 %copy-start.1 = (f32[8,64,384]{2,1,0:T(8,128)S(1)}, f32[8,64,384]{2,1,0:T(8,128)}, u32[]{:S(2)}) copy-start(f32[8,64,384]{2,1,0:T(8,128)} %param.15) | copy-start | bytes 2359300
  54.2 37.0 %copy-start.2 = (f32[8,64,64]{2,1,0:T(8,128)S(1)}, f32[8,64,64]{2,1,0:T(8,128)}, u32[]{:S(2)}) copy-start(f32[8,64,64]{2,1,0:T(8,128)} %param.16) | copy-start | bytes 393220
  54.2 46.6 %copy-start.5 = (s32[1,4]{1,0:T(1,128)S(1)}, s32[1,4]{1,0:T(1,128)}, u32[]{:S(2)}) copy-start(s32[1,4]{1,0:T(1,128)} %param.17) | copy-start | bytes 52
  54.2 46.8 %copy-start.4 = (f32[1,4,64,64]{3,2,1,0:T(8,128)S(1)}, f32[1,4,64,64]{3,2,1,0:T(8,128)}, u32[]{:S(2)}) copy-start(f32[1,4,64,64]{3,2,1,0:T(8,128)} %param.18) | copy-start | bytes 196612
  54.2 47.0 %copy-start.3 = (f32[8,64,64]{2,1,0:T(8,128)S(1)}, f32[8,64,64]{2,1,0:T(8,128)}, u32[]{:S(2)}) copy-start(f32[8,64,64]{2,1,0:T(8,128)} %param.19) | copy-start | bytes 393220
  89.4 12.6 %collective-permute-start.3 = (bf16[8,16,384]{2,1,0:T(8,128)(2,1)S(1)}, bf16[8,16,384]{2,1,0:T(8,128)(2,1)S(1)}, u32[]{:S(2)}, u32[]{:S(2)}) collective-permute-start(bf16[8,16,384]{2,1,0:T(8,128)(2,1)S(1)} %get-tuple-element.4), channel_id=1, source_target_pairs={{4,0},{8,4},{12,8},{16,12},{20,16},{24,20},{28,24},{0,28},{5,1},{9... | collective-permute-start | bytes 294920 | tf_op jit(solution)/shard_map/ppermute | solution.py:19
  89.4 12.5 %collective-permute-start.2 = (bf16[8,16,384]{2,1,0:T(8,128)(2,1)S(1)}, bf16[8,16,384]{2,1,0:T(8,128)(2,1)S(1)}, u32[]{:S(2)}, u32[]{:S(2)}) collective-permute-start(bf16[8,16,384]{2,1,0:T(8,128)(2,1)S(1)} %get-tuple-element.4), channel_id=1, source_target_pairs={{0,4},{4,8},{8,12},{12,16},{16,20},{20,24},{24,28},{28,0},{1,5},{5... | collective-permute-start | bytes 294920 | tf_op jit(solution)/shard_map/ppermute | solution.py:16
